TPU v7x, 32 devices: a whole 2x2x4 slice. The times are simulated.
32 devices in a mesh: seq: 16 (over z, y, x), head: 2 (over core).
Axes of the slice: x: 2, y: 2, z: 4, core: 2. Of those that a mesh axis runs over, the one named last changes fastest.
Arguments:
- hidden_in: bfloat16 [4, 16384], P(None, 'seq'), may hold values from -12 to 12
- norm_gain: float32 [16384], P('seq'), may hold values from 0.25 to 1.75
- qkv_codes: int32 [16384, 4608], P('seq', 'head'), may hold values from 0 to 255
- qkv_scale: float32 [18432], P('head'), may hold values from 0.00390625 to 0.015625
- out_codes: int32 [16384, 4096], P('seq', 'head'), may hold values from 0 to 255
- out_scale: float32 [16384], P('seq'), may hold values from 0.0078125 to 0.03125
- cache_keys: bfloat16 [4, 16384, 8, 128], P(None, 'seq', 'head'), may hold values from -200 to 200
- cache_values: bfloat16 [4, 16384, 8, 128], P(None, 'seq', 'head'), may hold values from -6 to 6
- lengths: int32 [4], replicated, may hold values from 8192 to 16384, as said below
Outputs:
- hidden_out: bfloat16 [4, 16384], P(None, 'seq')
Inputs may be any that keep to these rules, and one draw needn't show every extreme that they name: `lengths`: some sequence uses all 16384 cached positions in every draw.
All inputs are finite; a program needn't handle non-finite values.
Results may differ from a plain program's by a relative error of at most 0.02.
The roundings to bfloat16 on the way count: a program that leaves them out, or rounds other values in their place, can miss the bound.
Values sent between devices are 32-bit elements; how exact they have to be, the bound alone decides.
A program may use at most 192 MiB of HBM per device.

v0:
```python
import math

import jax
import jax.numpy as jnp
import numpy as np
from jax import lax
from jax.experimental import pallas as pl
from jax.experimental.pallas import tpu as pltpu
from jax.sharding import PartitionSpec as P

D = 16384
HEADS = 128
KV_HEADS = 8
HEAD_DIM = 128
TILE = 128
DECODE_STEPS = 2


code_norm = 147.8
epsilon = 1e-05
rope_base = 500000.0


LANES = 128
ROW_STEP = 32


def next_byte(values):
    lane = lax.broadcasted_iota(jnp.int32, values.shape, 1)
    tile_bytes = TILE // 4
    inside = pltpu.roll(values, LANES - 1, 1)
    wrapped = pltpu.roll(values, tile_bytes - 1, 1)
    return jnp.where(lane % tile_bytes == tile_bytes - 1, wrapped, inside)


def decode_kernel(scale_by_row, codes_ref, scale_ref, out_ref):
    width = codes_ref.shape[1]

    def row_step(index, carry):
        rows = pl.ds(pl.multiple_of(index * ROW_STEP, ROW_STEP), ROW_STEP)
        if scale_by_row:
            scale = scale_ref[rows, :]
        for chunk in range(width // LANES):
            first = codes_ref[rows, chunk * LANES : (chunk + 1) * LANES]
            pair = first * 256 + next_byte(first)
            window = pair * 256 + next_byte(next_byte(first))
            for phase in range(4):
                state = lax.shift_right_logical(window, 8 - 2 * phase) & 65535
                hashed = state * 34038481 + 76625530
                halves = (hashed & 0x00FF00FF) + (
                    lax.shift_right_logical(hashed, 8) & 0x00FF00FF
                )
                total = (halves & 0xFFFF) + lax.shift_right_logical(halves, 16)
                centred = (total - 510).astype(jnp.float32)
                start = phase * width + chunk * LANES
                if not scale_by_row:
                    scale = scale_ref[0:1, start : start + LANES]
                out_ref[rows, start : start + LANES] = (centred * scale).astype(jnp.bfloat16)
        return carry

    lax.fori_loop(0, codes_ref.shape[0] // ROW_STEP, row_step, 0)


def decode_weights(codes, scale, scale_by_row):
    rows, width = codes.shape
    block = math.gcd(rows, 128)
    if scale_by_row:
        scale_spec = pl.BlockSpec((block, LANES), lambda i: (i, 0))
    else:
        scale_spec = pl.BlockSpec((1, 4 * width), lambda i: (0, 0))
    return pl.pallas_call(
        lambda *refs: decode_kernel(scale_by_row, *refs),
        grid=(rows // block,),
        in_specs=[pl.BlockSpec((block, width), lambda i: (i, 0)), scale_spec],
        out_specs=pl.BlockSpec((block, 4 * width), lambda i: (i, 0)),
        out_shape=jax.ShapeDtypeStruct((rows, 4 * width), jnp.bfloat16),
        compiler_params=pltpu.CompilerParams(dimension_semantics=("arbitrary",)),
        cost_estimate=pl.CostEstimate(
            flops=rows * width * 80, bytes_accessed=rows * width * 12, transcendentals=0
        ),
    )(codes, scale)


def by_phase(values, width):
    split = values.reshape(values.shape[:-1] + (values.shape[-1] // 4, 4))
    split = jnp.swapaxes(split, -1, -2)
    padding = [(0, 0)] * (split.ndim - 1) + [(0, width - split.shape[-1])]
    return jnp.pad(split, padding).reshape(values.shape[:-1] + (4 * width,))


def from_phase(values, count):
    split = values.reshape(values.shape[0], 4, -1)[:, :, :count]
    return jnp.swapaxes(split, 1, 2).reshape(values.shape[0], 4 * count)


def padded_codes(codes):
    extra = -codes.shape[1] % LANES
    return jnp.pad(codes, ((0, 0), (0, extra))) if extra else codes


def rope_tables(positions):
    half_dim = HEAD_DIM // 2
    freqs = jnp.exp(
        -(jnp.arange(half_dim, dtype=jnp.float32) * (2.0 / HEAD_DIM)) * math.log(rope_base)
    )
    angles = positions.astype(jnp.float32)[:, None] * freqs[None, :]
    return (jnp.cos(angles), jnp.sin(angles))


def rotate(values, cosine_table, sine_table):
    half_dim = values.shape[-1] // 2
    first_half = values[..., :half_dim]
    second = values[..., half_dim:]
    return jnp.concatenate(
        [
            first_half * cosine_table - second * sine_table,
            second * cosine_table + first_half * sine_table,
        ],
        axis=-1,
    )


def finish(top_max, denominator, numerator, queries, new_keys, new_values):
    score_scale = HEAD_DIM ** (-0.5)
    query_float = queries.astype(jnp.float32)
    new_scores = [
        jnp.sum(query_float * new_key.astype(jnp.float32)[:, :, None, :], axis=-1) * score_scale
        for new_key in new_keys
    ]
    peak_score = top_max
    for new_score in new_scores:
        peak_score = jnp.maximum(peak_score, new_score)
    factor = jnp.exp(top_max - peak_score)
    denominator = denominator * factor
    numerator = numerator * factor[..., None]
    for new_score, new_value in zip(new_scores, new_values):
        weight_new = jnp.exp(new_score - peak_score)
        denominator = denominator + weight_new
        numerator = numerator + weight_new[..., None] * new_value.astype(jnp.float32)[:, :, None, :]
    attended = numerator / denominator[..., None]
    return attended.astype(jnp.bfloat16).reshape(attended.shape[0], -1)


def add_pieces(pieces):
    total = pieces[0]
    for piece in pieces[1:]:
        total = total + piece
    return total


def merge_pieces(pieces):
    half = HEAD_DIM // 2
    tops = [piece[:, HEAD_DIM : HEAD_DIM + 1] for piece in pieces]
    sums = [piece[:, HEAD_DIM + half : HEAD_DIM + half + 1] for piece in pieces]
    top_max = tops[0]
    for top in tops[1:]:
        top_max = jnp.maximum(top_max, top)
    numerator = jnp.zeros((pieces[0].shape[0], HEAD_DIM), jnp.float32)
    denominator = jnp.zeros((pieces[0].shape[0], 1), jnp.float32)
    for piece, top, part in zip(pieces, tops, sums):
        factor = jnp.exp(top - top_max)
        numerator = numerator + piece[:, :HEAD_DIM] * factor
        denominator = denominator + part * factor
    lane = lax.broadcasted_iota(jnp.int32, numerator.shape, 1)
    packed = jnp.where(lane < half, top_max, denominator)
    return jnp.concatenate([numerator, packed], axis=1)


def exchange_kernel(
    count, combine, in_ref, out_ref, arrived, gathered, send_one, recv_one, send_two, recv_two
):
    me = lax.axis_index("seq")
    head = lax.axis_index("head")
    barrier = pltpu.get_barrier_semaphore()
    for step in range(1, count):
        pl.semaphore_signal(
            barrier,
            inc=1,
            device_id=(lax.rem(me + step, count), head),
            device_id_type=pl.DeviceIdType.MESH,
        )
    pl.semaphore_wait(barrier, count - 1)
    first = []
    for step in range(1, count):
        target = lax.rem(me + step, count)
        copy = pltpu.make_async_remote_copy(
            src_ref=in_ref.at[target],
            dst_ref=arrived.at[step],
            send_sem=send_one.at[step],
            recv_sem=recv_one.at[step],
            device_id=(target, head),
            device_id_type=pl.DeviceIdType.MESH,
        )
        copy.start()
        first.append(copy)
    for copy in first:
        copy.wait_recv()
    pieces = [in_ref[me]] + [arrived[step] for step in range(1, count)]
    gathered[0] = combine(pieces)
    second = []
    for step in range(1, count):
        copy = pltpu.make_async_remote_copy(
            src_ref=gathered.at[0],
            dst_ref=gathered.at[step],
            send_sem=send_two.at[step],
            recv_sem=recv_two.at[step],
            device_id=(lax.rem(me + step, count), head),
            device_id_type=pl.DeviceIdType.MESH,
        )
        copy.start()
        second.append(copy)
    out_ref[me] = gathered[0]
    for copy in first:
        copy.wait_send()
    for step, copy in enumerate(second, 1):
        copy.wait_recv()
        out_ref[lax.rem(me + count - step, count)] = gathered[step]
    for copy in second:
        copy.wait_send()


def exchange(values, combine, collective_id):
    count = values.shape[0]
    return pl.pallas_call(
        lambda *refs: exchange_kernel(count, combine, *refs),
        in_specs=[pl.BlockSpec(memory_space=pltpu.VMEM)],
        out_specs=pl.BlockSpec(memory_space=pltpu.VMEM),
        out_shape=jax.ShapeDtypeStruct(values.shape, values.dtype),
        scratch_shapes=[
            pltpu.VMEM(values.shape, values.dtype),
            pltpu.VMEM(values.shape, values.dtype),
        ]
        + [pltpu.SemaphoreType.DMA((count,))] * 4,
        compiler_params=pltpu.CompilerParams(collective_id=collective_id, has_side_effects=True),
    )(values)


def sum_over_seq(partial_value, squares):
    count = lax.axis_size("seq")
    rows, columns = partial_value.shape
    chunk = -(-(columns + LANES) // (count * LANES)) * LANES
    packed = jnp.concatenate(
        [
            partial_value,
            jnp.broadcast_to(squares[:, None], (rows, count * chunk - columns)),
        ],
        axis=1,
    )
    packed = jnp.swapaxes(packed.reshape(rows, count, chunk), 0, 1)
    packed = exchange(packed, add_pieces, 0)
    packed = jnp.swapaxes(packed, 0, 1).reshape(rows, count * chunk)
    return packed[:, :columns], packed[:, columns]


def merge_over_seq(local_max, local_sum, local_acc):
    count = lax.axis_size("seq")
    half = local_acc.shape[:-1] + (HEAD_DIM // 2,)
    packed = jnp.concatenate(
        [
            local_acc,
            jnp.broadcast_to(local_max[..., None], half),
            jnp.broadcast_to(local_sum[..., None], half),
        ],
        axis=-1,
    ).reshape(count, -1, 2 * HEAD_DIM)
    packed = exchange(packed, merge_pieces, 1).reshape(local_acc.shape[:-1] + (2 * HEAD_DIM,))
    return packed[..., HEAD_DIM], packed[..., 3 * HEAD_DIM // 2], packed[..., :HEAD_DIM]


def shards(
    hidden_in,
    norm_gain,
    qkv_codes,
    qkv_scale,
    out_codes,
    out_scale,
    cache_keys,
    cache_values,
    lengths,
):
    score_scale = HEAD_DIM ** (-0.5)
    groups = HEADS // KV_HEADS
    qkv_bytes = qkv_codes.shape[1]
    qkv_codes = padded_codes(qkv_codes)
    out_codes = padded_codes(out_codes)
    qkv_width = qkv_codes.shape[1]
    out_width = out_codes.shape[1]
    w_qkv = decode_weights(
        qkv_codes, by_phase((qkv_scale / code_norm)[None, :], qkv_width), False
    )
    row_scale = jnp.broadcast_to((out_scale / code_norm)[:, None], (out_scale.shape[0], LANES))
    w_out = decode_weights(out_codes, row_scale, True)
    batch_size = cache_keys.shape[0]
    block_len = cache_keys.shape[1]
    group_count = cache_keys.shape[2]
    shard_start = lax.axis_index("seq") * block_len
    live_mask = (shard_start + jnp.arange(block_len, dtype=jnp.int32))[None, :] < lengths[:, None]
    live_mask = live_mask[:, None, None, :]
    hidden = hidden_in
    new_keys = []
    new_values = []
    for decode_step in range(DECODE_STEPS):
        positions = lengths + decode_step
        squares = jnp.sum(jnp.square(hidden.astype(jnp.float32)), axis=1)
        normed = (hidden.astype(jnp.float32) * norm_gain[None, :]).astype(jnp.bfloat16)
        partial_value = jnp.dot(normed, w_qkv, preferred_element_type=jnp.float32)
        partial_value, squares = sum_over_seq(partial_value, squares)
        partial_value = from_phase(partial_value, qkv_bytes)
        projected = partial_value * lax.rsqrt(squares / D + epsilon)[:, None]
        grouped = projected.reshape(batch_size, group_count, groups + 2, HEAD_DIM)
        cosine_table, sine_table = rope_tables(positions)
        queries = rotate(
            grouped[:, :, :groups], cosine_table[:, None, None, :], sine_table[:, None, None, :]
        ).astype(jnp.bfloat16)
        new_keys.append(
            rotate(grouped[:, :, groups], cosine_table[:, None, :], sine_table[:, None, :]).astype(
                jnp.bfloat16
            )
        )
        new_values.append(grouped[:, :, groups + 1].astype(jnp.bfloat16))
        scores = (
            jnp.einsum("bgrd,bcgd->bgrc", queries, cache_keys, preferred_element_type=jnp.float32)
            * score_scale
        )
        local_max = jnp.max(jnp.where(live_mask, scores, -1e30), axis=3)
        weights = jnp.where(live_mask, jnp.exp(scores - local_max[..., None]), 0.0)
        local_sum = jnp.sum(weights, axis=3)
        local_acc = jnp.einsum(
            "bgrc,bcgd->bgrd",
            weights.astype(jnp.bfloat16),
            cache_values,
            preferred_element_type=jnp.float32,
        )
        top_max, denominator, numerator = merge_over_seq(local_max, local_sum, local_acc)
        attended = finish(top_max, denominator, numerator, queries, new_keys, new_values)
        update = lax.dot_general(
            by_phase(attended, out_width), w_out, (((1,), (1,)), ((), ())), preferred_element_type=jnp.float32
        )
        update = lax.psum(update, "head")
        hidden = (hidden.astype(jnp.float32) + update).astype(jnp.bfloat16)
    return hidden


def solution(mesh):
    in_specs = (
        P(None, "seq"),
        P("seq"),
        P("seq", "head"),
        P("head"),
        P("seq", "head"),
        P("seq"),
        P(None, "seq", "head", None),
        P(None, "seq", "head", None),
        P(),
    )
    out_specs = P(None, "seq")
    return jax.shard_map(shards, mesh=mesh, in_specs=in_specs, out_specs=out_specs, check_vma=False)
```

profile of v0, /device:TPU:0, one launch (start us, length us, event | category | flops | bytes accessed | tf_op | source)
XLA Modules:
  0.0 262.2 jit_solution(3499406418605702273)
XLA Ops:
  0.8 1.2 reshape_broadcast_in_dim.3
  3.0 48.3 %shard_map.91 = bf16[1024,9216]{1,0:T(8,128)(2,1)} custom-call(s32[1024,2304]{1,0:T(8,128)} %refs_0_.2, f32[1,9216]{1,0:T(1,128)} %bitcast.123), custom_call_target="tpu_custom_call" | custom-call | flops 188743680 | bytes 28311552 | tf_op jit(solution)/shard_map/pallas_call | solution.py:71
  51.3 8.9 %fusion.45 = f32[4,9216]{1,0:T(4,128)S(1)} fusion(bf16[1024,9216]{1,0:T(8,128)(2,1)} %shard_map.91, bf16[4,1024]{1,0:T(4,128)(2,1)S(1)} %copy-done.1, f32[1024]{0:T(1024)S(1)} %copy-done), kind=kOutput, calls=%fused_computation.68 | convolution fusion | flops 75509760 | bytes 19034112 | tf_op jit(solution)/shard_map/dot_general | solution.py:306
  61.1 19.9 %shard_map.92 = f32[16,4,640]{2,1,0:T(4,128)} custom-call(f32[16,4,640]{2,1,0:T(4,128)} %bitcast.113), custom_call_target="tpu_custom_call" | custom-call | tf_op jit(solution)/shard_map/pallas_call | solution.py:224
  82.1 2.9 %copy.34 = f32[4,4,2304]{1,2,0:T(8,128)} copy(f32[4,4,2304]{2,1,0:T(4,128)S(1)} %reshape.347) | data formatting | bytes 294912 | tf_op jit(solution)/shard_map/reshape | solution.py:92
  85.0 5.1 %reshape.348 = f32[4,4,18,128]{3,2,1,0:T(8,128)S(1)} reshape(f32[4,2304,4]{2,1,0:T(8,128)} %bitcast.102) | data formatting | bytes 294912 | tf_op jit(solution)/shard_map/reshape | solution.py:93
  91.4 3.7 %select_reduce_fusion.1 = (f32[4,4,16]{2,1,0:T(4,128)S(1)}, f32[4,4,16,1024]{3,2,1,0:T(8,128)S(1)}) fusion(pred[4,1024]{1,0:T(4,128)(4,1)S(1)} %broadcast_compare_fusion, bf16[4,1024,4,128]{3,2,1,0:T(4,128)(2,1)} %param.15, bf16[4,4,16,64]{3,2,1,0:T(8,128)(2,1)S(1)} %get-tuple-element.16, bf16[4,4,16,64]{3,2,1,0:T(8,128)(2,1)S(1)} %get-tuple-element.15), kind=kOutput, calls=%fused_computation.13 | convolution fusion | flops 68026112 | bytes 5313536 | tf_op jit(solution)/shard_map/bgrd,bcgd->bgrc/dot_general | solution.py:322
  97.4 17.7 %shard_map.93 = f32[16,16,256]{2,1,0:T(8,128)} custom-call(f32[16,16,256]{2,1,0:T(8,128)} %bitcast.111), custom_call_target="tpu_custom_call" | custom-call | tf_op jit(solution)/shard_map/pallas_call | solution.py:224
  115.1 1.1 fusion.69
  116.9 1.1 fusion.33
  118.0 4.5 %reshape_reshape.6 = bf16[4,2048,4]{2,1,0:T(8,128)(2,1)S(1)} reshape(bf16[4,4,16,128]{3,2,1,0:T(8,128)(2,1)S(1)} %fusion.33) | data formatting | bytes 131072 | tf_op jit(solution)/shard_map/reshape;reshape | solution.py:85
  124.5 41.6 %shard_map.94 = bf16[1024,8192]{1,0:T(8,128)(2,1)} custom-call(s32[1024,2048]{1,0:T(8,128)} %refs_0_.3, f32[1024,128]{1,0:T(8,128)} %broadcast_in_dim.46.refs_1_), custom_call_target="tpu_custom_call" | custom-call | flops 167772160 | bytes 25165824 | tf_op jit(solution)/shard_map/pallas_call | solution.py:71
  166.1 10.2 %fusion.70 = f32[4,1024]{1,0:T(4,128)S(1)} fusion(bf16[4,8192]{1,0:T(4,128)(2,1)S(1)} %bitcast.119, bf16[1024,8192]{1,0:T(8,128)(2,1)} %shard_map.94), kind=kOutput, calls=%fused_computation.117 | convolution fusion | flops 67108864 | bytes 16859136 | tf_op jit(solution)/shard_map/dot_general | solution.py:336
  176.3 3.4 %psum.14 = f32[4,1024]{1,0:T(4,128)S(1)} all-reduce(f32[4,1024]{1,0:T(4,128)S(1)} %fusion.70), channel_id=1, replica_groups=mesh['seq'=16,'head'=2] {'head'}, use_global_device_ids=true, to_apply=%region_4.5 | all-reduce | flops 4096 | bytes 32768 | tf_op jit(solution)/shard_map/psum | solution.py:339
  179.8 8.9 %fusion.43 = f32[4,9216]{1,0:T(4,128)S(1)} fusion(bf16[1024,9216]{1,0:T(8,128)(2,1)} %shard_map.91, bf16[4,1024]{1,0:T(4,128)(2,1)S(1)} %get-tuple-element.8, f32[1024]{0:T(1024)S(1)} %copy-done), kind=kOutput, calls=%fused_computation.67 | convolution fusion | flops 75509760 | bytes 19034112 | tf_op jit(solution)/shard_map/dot_general | solution.py:306
  189.5 16.5 %shard_map.95 = f32[16,4,640]{2,1,0:T(4,128)} custom-call(f32[16,4,640]{2,1,0:T(4,128)} %bitcast.114), custom_call_target="tpu_custom_call" | custom-call | tf_op jit(solution)/shard_map/pallas_call | solution.py:224
  207.0 3.1 %copy.40 = f32[4,4,2304]{1,2,0:T(8,128)} copy(f32[4,4,2304]{2,1,0:T(4,128)S(1)} %reshape.354) | data formatting | bytes 294912 | tf_op jit(solution)/shard_map/reshape | solution.py:92
  210.1 5.1 %reshape.355 = f32[4,4,18,128]{3,2,1,0:T(8,128)S(1)} reshape(f32[4,2304,4]{2,1,0:T(8,128)} %bitcast.103) | data formatting | bytes 294912 | tf_op jit(solution)/shard_map/reshape | solution.py:93
  216.8 3.5 %select_reduce_fusion = (f32[4,4,16]{2,1,0:T(4,128)S(1)}, f32[4,4,16,1024]{3,2,1,0:T(8,128)S(1)}) fusion(pred[4,1024]{1,0:T(4,128)(4,1)S(1)} %broadcast_compare_fusion, bf16[4,1024,4,128]{3,2,1,0:T(4,128)(2,1)} %param.15, bf16[4,4,16,64]{3,2,1,0:T(8,128)(2,1)S(1)} %get-tuple-element.14, bf16[4,4,16,64]{3,2,1,0:T(8,128)(2,1)S(1)} %get-tuple-element.13), kind=kOutput, calls=%fused_computation.11 | convolution fusion | flops 68026112 | bytes 5313536 | tf_op jit(solution)/shard_map/bgrd,bcgd->bgrc/dot_general | solution.py:322
  222.6 17.3 %shard_map.96 = f32[16,16,256]{2,1,0:T(8,128)} custom-call(f32[16,16,256]{2,1,0:T(8,128)} %bitcast.112), custom_call_target="tpu_custom_call" | custom-call | tf_op jit(solution)/shard_map/pallas_call | solution.py:224
  241.4 1.1 fusion.34
  242.5 4.5 %reshape_reshape.7 = bf16[4,2048,4]{2,1,0:T(8,128)(2,1)S(1)} reshape(bf16[4,4,16,128]{3,2,1,0:T(8,128)(2,1)S(1)} %fusion.34) | data formatting | bytes 131072 | tf_op jit(solution)/shard_map/reshape;reshape | solution.py:85
  248.0 10.2 %fusion.71 = f32[4,1024]{1,0:T(4,128)S(1)} fusion(bf16[4,8192]{1,0:T(4,128)(2,1)S(1)} %bitcast.120, bf16[1024,8192]{1,0:T(8,128)(2,1)} %shard_map.94), kind=kOutput, calls=%fused_computation.118 | convolution fusion | flops 67108864 | bytes 16859136 | tf_op jit(solution)/shard_map/dot_general | solution.py:336
  258.2 3.4 %psum.15 = f32[4,1024]{1,0:T(4,128)S(1)} all-reduce(f32[4,1024]{1,0:T(4,128)S(1)} %fusion.71), channel_id=1, replica_groups=mesh['seq'=16,'head'=2] {'head'}, use_global_device_ids=true, to_apply=%region_10.11 | all-reduce | flops 4096 | bytes 32768 | tf_op jit(solution)/shard_map/psum | solution.py:339
  (70 shorter events, 18.8 us)
Async XLA Ops:
  3.0 48.3 %copy-start = (f32[1024]{0:T(1024)S(1)}, f32[1024]{0:T(1024)}, u32[]{:S(2)}) copy-start(f32[1024]{0:T(1024)} %param.10) | copy-start | bytes 12292
  3.0 48.3 %copy-start.1 = (bf16[4,1024]{1,0:T(4,128)(2,1)S(1)}, bf16[4,1024]{1,0:T(4,128)(2,1)}, u32[]{:S(2)}) copy-start(bf16[4,1024]{1,0:T(4,128)(2,1)} %param.9) | copy-start | bytes 24580
  82.1 8.9 %copy-start.3 = (s32[4]{0:T(128)S(1)}, s32[4]{0:T(128)}, u32[]{:S(2)}) copy-start(s32[4]{0:T(128)} %param.17) | copy-start | bytes 52
  91.3 3.8 %copy-start.4 = (bf16[4,1024,4,128]{3,2,1,0:T(4,128)(2,1)S(1)}, bf16[4,1024,4,128]{3,2,1,0:T(4,128)(2,1)}, u32[]{:S(2)}) copy-start(bf16[4,1024,4,128]{3,2,1,0:T(4,128)(2,1)} %param.16) | copy-start | bytes 12582916
  96.0 27.5 %copy-start.2 = (f32[1024]{0:T(1024)S(1)}, f32[1024]{0:T(1024)}, u32[]{:S(2)}) copy-start(f32[1024]{0:T(1024)} %param.14) | copy-start | bytes 12292
  215.2 5.1 %copy-start.5 = (bf16[4,1024,4,128]{3,2,1,0:T(4,128)(2,1)S(1)}, bf16[4,1024,4,128]{3,2,1,0:T(4,128)(2,1)}, u32[]{:S(2)}) copy-start(bf16[4,1024,4,128]{3,2,1,0:T(4,128)(2,1)} %param.16) | copy-start | bytes 12582916
where the time goes:
time: 263 us; the launch traced here: 262 us
  Pallas kernels  161 us (61%)
  matrix products  47.4 us (18%)
  local copies, waits for them, and re-layouts  35.8 us (14%)
  other arithmetic  10.7 us (4%)
  blocking collectives  6.73 us (3%)
    pallas_call x2, Pallas kernels, decode_weights(): pl.pallas_call(lambda *refs: decode_kernel(scale_by_row, *refs), grid=(ro...  89.9 us
    pallas_call x4, Pallas kernels, exchange(): pl.pallas_call(lambda *refs: exchange_kernel(count, combine, *refs), in_s...  71.3 us
    dot_general x2, matrix products, shards(): lax.dot_general(by_phase(attended, out_width), w_out, (((1,), (1,)), ((),...  20.4 us
    dot_general x2, matrix products, shards(): partial_value = jnp.dot(normed, w_qkv, preferred_element_type=jnp.float32)  17.8 us
    another operation x3, local copies, waits for them, and re-layouts, by_phase(): split = values.reshape(values.shape[:-1] + (values.shape[-1] // 4, 4))  10.2 us
    reshape x2, local copies, waits for them, and re-layouts, from_phase(): return jnp.swapaxes(split, 1, 2).reshape(values.shape[0], 4 * count)  10.2 us
    dot_general x2, matrix products, shards(): jnp.einsum('bgrd,bcgd->bgrc', queries, cache_keys, preferred_element_type...  7.18 us
    psum x2, blocking collectives, shards(): update = lax.psum(update, 'head')  6.73 us

commit v1 on v0

v1 whole, which is shorter than its diff:
```python
import functools
import math

import jax
import jax.numpy as jnp
from jax import lax
from jax.experimental import pallas as pl
from jax.experimental.pallas import tpu as pltpu
from jax.sharding import PartitionSpec as P

HEADS = 128
KV_HEADS = 8
HEAD_DIM = 128
TILE = 128
DECODE_STEPS = 2

code_norm = 147.8
epsilon = 1e-05
rope_base = 500000.0

LANES = 128
WIDE = 4 * LANES
GROUP = HEADS // KV_HEADS
PER_KV = GROUP + 2
TILE_BYTES = TILE // 4
ROWS = 128
DEPTH = 3
BYTES = 0x00FF00FF
LOW = -1e30
MESH = pl.DeviceIdType.MESH
NT = (((1,), (1,)), ((), ()))


def byte_windows(first):
    lane = lax.broadcasted_iota(jnp.int32, first.shape, 1)
    base = lane & ~(TILE_BYTES - 1)
    one = base | ((lane + 1) & (TILE_BYTES - 1))
    two = base | ((lane + 2) & (TILE_BYTES - 1))
    second = jnp.take_along_axis(first, one, axis=1)
    third = jnp.take_along_axis(first, two, axis=1)
    return (((first << 8) | second) << 8) | third


def hashed_weight(window, phase):
    state = lax.shift_right_logical(window, 8 - 2 * phase)
    if phase:
        state = state & 65535
    hashed = state * 34038481 + 76625530
    halves = (hashed & BYTES) + (lax.shift_right_logical(hashed, 8) & BYTES)
    total = lax.shift_right_logical(halves * 65537, 16) - 510
    return total.astype(jnp.float32).astype(jnp.bfloat16)


class Stream:
    def __init__(self, codes, buf, win, sem, weights):
        self.codes, self.buf, self.win, self.sem, self.weights = codes, buf, win, sem, weights
        self.count = codes.shape[1] // LANES
        self.rows = codes.shape[0]
        self.block = math.gcd(ROWS, self.rows)
        self.steps = self.rows // self.block

    def copy(self, chunk):
        slot = lax.rem(chunk, DEPTH)
        column = pl.multiple_of(chunk * LANES, LANES)
        return pltpu.make_async_copy(
            self.codes.at[:, pl.ds(column, LANES)], self.buf.at[slot], self.sem.at[slot]
        )

    def begin(self):
        for chunk in range(min(DEPTH, self.count)):
            self.copy(chunk).start()

    def block_rows(self, step):
        return pl.ds(pl.multiple_of(step * self.block, self.block), self.block)

    def first_windows(self):
        self.copy(0).wait()

        def body(step, carry):
            rows = self.block_rows(step)
            self.win[0, rows, :] = byte_windows(self.buf[0, rows, :])
            return carry

        lax.fori_loop(0, self.steps, body, 0)

    def chunk(self, chunk, beside=None):
        now, later = lax.rem(chunk, 2), lax.rem(chunk + 1, 2)
        slot = lax.rem(chunk + 1, DEPTH)

        @pl.when(chunk + 1 < self.count)
        def _():
            self.copy(chunk + 1).wait()

        @pl.when(chunk + DEPTH < self.count)
        def _():
            self.copy(chunk + DEPTH).start()

        def body(step, carry):
            rows = self.block_rows(step)
            if beside is not None:
                beside(chunk, step, rows)
            window = self.win[now, rows, :]
            for phase in range(4):
                self.weights[chunk, phase, rows, :] = hashed_weight(window, phase)
            self.win[later, rows, :] = byte_windows(self.buf[slot, rows, :])
            return carry

        lax.fori_loop(0, self.steps, body, 0)

    def run(self, low, high):
        def body(chunk, carry):
            self.chunk(chunk)
            return carry

        if high > low:
            lax.fori_loop(low, high, body, 0)


def kernel(
    hidden_ref,
    gain_ref,
    qkv_codes,
    qkv_scale,
    out_codes,
    out_scale,
    keys_hbm,
    values_hbm,
    lengths,
    cosine,
    sine,
    out_ref,
    w_qkv,
    w_out,
    qkv_buf,
    qkv_win,
    out_buf,
    out_win,
    keys,
    values,
    perm,
    padded,
    normed,
    hidden,
    accum,
    part,
    stage,
    owned_scale,
    square_all,
    arrived,
    heads_all,
    scores,
    merge_send,
    merge_arrived,
    attended,
    attended_own,
    by_phase,
    share,
    share_arrived,
    qkv_sem,
    out_sem,
    cache_sem,
    square_send_sem,
    square_sem,
    part_send_sem,
    part_sem,
    heads_send_sem,
    heads_sem,
    merge_send_sem,
    merge_sem,
    attended_send_sem,
    attended_sem,
    share_send_sem,
    share_sem,
):
    count = lax.axis_size("seq")
    head_count = lax.axis_size("head")
    me = lax.axis_index("seq")
    head = lax.axis_index("head")
    batch, depth = hidden_ref.shape
    features = depth * count
    chunks = w_qkv.shape[0]
    out_chunks = w_out.shape[0]
    owners = -(-chunks // count)
    cached = keys.shape[1]
    head_rows = attended.shape[1]
    groups = head_rows // GROUP
    block_len = cached // groups
    rows_each = merge_send.shape[1] - 1
    score_scale = HEAD_DIM ** (-0.5)

    def peer(step):
        return lax.rem(me + step, count)

    qkv = Stream(qkv_codes, qkv_buf, qkv_win, qkv_sem, w_qkv)
    outs = Stream(out_codes, out_buf, out_win, out_sem, w_out)
    qkv.begin()
    barrier = pltpu.get_barrier_semaphore()
    for step in range(1, count):
        pl.semaphore_signal(barrier, inc=1, device_id=(peer(step), head), device_id_type=MESH)
    for step in range(1, head_count):
        other = lax.rem(head + step, head_count)
        pl.semaphore_signal(barrier, inc=1, device_id=(me, other), device_id_type=MESH)

    def build(step, carry):
        rows = pl.ds(pl.multiple_of(step * LANES, LANES), LANES)
        natural = lax.broadcasted_iota(jnp.int32, (LANES, WIDE), 0) + step * LANES
        lane = lax.broadcasted_iota(jnp.int32, (LANES, WIDE), 1)
        source = ((lane >> 5) & 3) * LANES + (lane & 31) * 4 + (lane >> 7)
        perm[rows, :] = jnp.where(natural == source, 1.0, 0.0).astype(jnp.bfloat16)
        return carry

    lax.fori_loop(0, 4, build, 0)
    stage[...] = jnp.zeros_like(stage)
    padded[...] = jnp.zeros_like(padded)
    attended[...] = jnp.zeros_like(attended)
    hidden[...] = hidden_ref[...].astype(jnp.float32)

    for index in range(owners):
        chunk = jnp.minimum(me + index * count, chunks - 1)
        column = pl.multiple_of(chunk * WIDE, WIDE)
        scale = qkv_scale[0:1, pl.ds(column, WIDE)] / code_norm
        high = scale.astype(jnp.bfloat16).astype(jnp.float32)
        middle = (scale - high).astype(jnp.bfloat16).astype(jnp.float32)
        low = scale - high - middle
        stage[0:1, :] = high
        stage[1:2, :] = middle
        stage[2:3, :] = low
        moved = jnp.dot(
            stage[...].astype(jnp.bfloat16), perm[...], preferred_element_type=jnp.float32
        )
        owned_scale[index] = jnp.broadcast_to(
            moved[0:1, :] + moved[1:2, :] + moved[2:3, :], (8, WIDE)
        )
    stage[...] = jnp.zeros_like(stage)

    def start_square_copies(step_index):
        for step in range(1, count):
            pltpu.make_async_remote_copy(
                src_ref=square_all.at[step_index, 0],
                dst_ref=square_all.at[step_index, step],
                send_sem=square_send_sem.at[step_index, step],
                recv_sem=square_sem.at[step_index, step],
                device_id=(peer(step), head),
                device_id_type=MESH,
            ).start()

    def square_copy(step_index, step):
        return pltpu.make_async_remote_copy(
            src_ref=square_all.at[step_index, 0],
            dst_ref=square_all.at[step_index, step],
            send_sem=square_send_sem.at[step_index, step],
            recv_sem=square_sem.at[step_index, step],
            device_id=(peer(step), head),
            device_id_type=MESH,
        )

    def begin_step(step_index):
        values_now = hidden[...]
        squares = jnp.sum(jnp.square(values_now), axis=1, keepdims=True)
        square_all[step_index, 0] = jnp.broadcast_to(squares, (batch, LANES))
        padded[0:batch, :] = values_now * gain_ref[...]
        normed[...] = padded[...].astype(jnp.bfloat16)

    def part_copy(step_index, chunk):
        owner = lax.rem(chunk, count)
        index = chunk // count
        offset = lax.rem(owner - me + count, count)
        return pltpu.make_async_remote_copy(
            src_ref=part.at[step_index, chunk],
            dst_ref=arrived.at[step_index, index, jnp.maximum(offset - 1, 0)],
            send_sem=part_send_sem.at[step_index, chunk],
            recv_sem=part_sem.at[step_index, index],
            device_id=(owner, head),
            device_id_type=MESH,
        )

    def send_part(step_index, chunk):
        @pl.when(lax.rem(chunk, count) != me)
        def _():
            part_copy(step_index, chunk).start()

    def qkv_product(chunk):
        weights = jnp.concatenate([w_qkv[chunk, phase] for phase in range(4)], axis=1)
        return jnp.dot(normed[...], weights, preferred_element_type=jnp.float32)

    def heads_copy(step_index, chunk, step):
        rows = pl.ds(pl.multiple_of(chunk * 16, 16), 16)
        return pltpu.make_async_remote_copy(
            src_ref=heads_all.at[step_index, rows, :],
            dst_ref=heads_all.at[step_index, rows, :],
            send_sem=heads_send_sem.at[step_index, chunk // count, step],
            recv_sem=heads_sem.at[step_index, chunk],
            device_id=(peer(step), head),
            device_id_type=MESH,
        )

    def finish_heads(step_index):
        for step in range(1, count):
            square_copy(step_index, step).wait_recv()
        squares = square_all[step_index, 0]
        for step in range(1, count):
            squares = squares + square_all[step_index, step]
        inverse = lax.rsqrt(squares / features + epsilon)
        lane = lax.broadcasted_iota(jnp.int32, (8, LANES), 1)
        lower = (lane & 31) < 16
        for index in range(owners):
            chunk = me + index * count

            def work(index=index, chunk=chunk):
                pieces = arrived.at[step_index, index]
                pltpu.make_async_copy(pieces, pieces, part_sem.at[step_index, index]).wait()
                total = part[step_index, chunk]
                for step in range(count - 1):
                    total = total + arrived[step_index, index, step]
                first = lax.rem(4 * chunk, PER_KV)
                place = first + (lane >> 5)
                place = jnp.where(place >= PER_KV, place - PER_KV, place)
                plain = place == PER_KV - 1
                for phase in range(4):
                    columns = slice(phase * LANES, (phase + 1) * LANES)
                    padded_inverse = inverse
                    stage[0:batch, columns] = total[:, columns] * padded_inverse
                    entry = stage[0:8, columns] * owned_scale[index, :, columns]
                    partner = jnp.where(
                        lower, pltpu.roll(entry, LANES - 16, 1), pltpu.roll(entry, 16, 1)
                    )
                    turned = (
                        entry * cosine[step_index, phase] + partner * sine[step_index, phase]
                    )
                    stage[0:8, columns] = jnp.where(plain, entry, turned)
                natural = lax.dot_general(
                    stage[...].astype(jnp.bfloat16),
                    perm[...],
                    NT,
                    preferred_element_type=jnp.float32,
                )
                for place_in in range(4):
                    accum[place_in * 4 : place_in * 4 + 4, 0:LANES] = natural[
                        0:4, place_in * LANES : (place_in + 1) * LANES
                    ]
                rows = pl.ds(pl.multiple_of(chunk * 16, 16), 16)
                heads_all[step_index, rows, :] = accum[:, 0:LANES]
                for step in range(1, count):
                    heads_copy(step_index, chunk, step).start()

            if (index + 1) * count <= chunks:
                work()
            else:
                pl.when(chunk < chunks)(work)

    def wait_heads(step_index):
        for chunk in range(chunks):

            @pl.when(me != chunk % count)
            def _(chunk=chunk):
                heads_copy(step_index, chunk, 1).wait_recv()

    def merge_copy(step_index, step):
        target = peer(step)
        return pltpu.make_async_remote_copy(
            src_ref=merge_send.at[step_index * count + target],
            dst_ref=merge_arrived.at[step_index, step],
            send_sem=merge_send_sem.at[step_index, step],
            recv_sem=merge_sem.at[step_index, step],
            device_id=(target, head),
            device_id_type=MESH,
        )

    def attend(step_index):
        wait_heads(step_index)
        column = lax.broadcasted_iota(jnp.int32, (head_rows, cached), 1)
        row = lax.broadcasted_iota(jnp.int32, (head_rows, cached), 0)
        if step_index == 0:
            for b in range(batch):
                pltpu.make_async_copy(keys_hbm.at[b], keys.at[b], cache_sem.at[0, b]).wait()
                pltpu.make_async_copy(values_hbm.at[b], values.at[b], cache_sem.at[1, b]).wait()
        width = math.gcd(cached, 1024)
        tiles = cached // width
        lane = lax.broadcasted_iota(jnp.int32, (head_rows, LANES), 1)
        line = lax.broadcasted_iota(jnp.int32, (head_rows, LANES), 0)
        for b in range(batch):
            query = jnp.concatenate(
                [
                    heads_all[step_index, pl.ds(g * PER_KV * 4 + b, GROUP, stride=4), :]
                    for g in range(groups)
                ],
                axis=0,
            ).astype(jnp.bfloat16)
            live_length = lengths[b] - me * block_len
            top = jnp.full((head_rows, 1), LOW, jnp.float32)
            for tile in range(tiles):
                columns = slice(tile * width, (tile + 1) * width)
                score = (
                    lax.dot_general(
                        query, keys[b, columns, :], NT, preferred_element_type=jnp.float32
                    )
                    * score_scale
                )
                position = lax.broadcasted_iota(jnp.int32, (head_rows, width), 1) + tile * width
                row_group = lax.broadcasted_iota(jnp.int32, (head_rows, width), 0) // GROUP
                live = position < live_length * groups
                if groups > 1:
                    live = live & (lax.rem(position, groups) == row_group)
                score = jnp.where(live, score, LOW)
                scores[b % 2, :, columns] = score
                top = jnp.maximum(top, jnp.max(score, axis=1, keepdims=True))
            total = jnp.zeros((head_rows, 1), jnp.float32)
            mixed = jnp.zeros((head_rows, HEAD_DIM), jnp.float32)
            for tile in range(tiles):
                columns = slice(tile * width, (tile + 1) * width)
                score = scores[b % 2, :, columns]
                weight = jnp.where(score > 0.5 * LOW, jnp.exp(score - top), 0.0)
                total = total + jnp.sum(weight, axis=1, keepdims=True)
                mixed = mixed + jnp.dot(
                    weight.astype(jnp.bfloat16),
                    values[b, columns, :],
                    preferred_element_type=jnp.float32,
                )
            spread = jnp.where(lane == line, top, 0.0) + jnp.where(
                lane == line + LANES // 2, total, 0.0
            )
            spread = jnp.sum(spread, axis=0, keepdims=True)
            each = head_rows // rows_each
            for piece in range(each):
                slot = step_index * count + b * each + piece
                merge_send[slot, 0:rows_each, :] = mixed[
                    piece * rows_each : (piece + 1) * rows_each, :
                ]
                merge_send[slot, rows_each : rows_each + 1, :] = spread
        for step in range(1, count):
            merge_copy(step_index, step).start()

    def attended_place():
        first = me * rows_each
        b = first // head_rows
        line = lax.rem(first, head_rows)
        return b, line

    def attended_copy(step_index, step):
        b, line = attended_place()
        return pltpu.make_async_remote_copy(
            src_ref=attended_own.at[step_index],
            dst_ref=attended.at[step_index, pl.ds(line, rows_each), b, :],
            send_sem=attended_send_sem.at[step_index, step],
            recv_sem=attended_sem.at[step_index],
            device_id=(peer(step), head),
            device_id_type=MESH,
        )

    def merge(step_index):
        for step in range(1, count):
            merge_copy(step_index, step).wait_recv()
        b, line = attended_place()
        own = step_index * count + me
        pieces = [merge_send[own, 0:rows_each, :]]
        stats = [merge_send[own, rows_each : rows_each + 1, :]]
        for step in range(1, count):
            pieces.append(merge_arrived[step_index, step, 0:rows_each, :])
            stats.append(merge_arrived[step_index, step, rows_each : rows_each + 1, :])
        top = stats[0]
        for stat in stats[1:]:
            top = jnp.maximum(top, stat)
        lane = lax.broadcasted_iota(jnp.int32, (rows_each, LANES), 1)
        row = lax.broadcasted_iota(jnp.int32, (rows_each, LANES), 0)
        chosen = lane == line + row

        def to_column(values_row):
            spread = jnp.where(chosen, jnp.broadcast_to(values_row, (rows_each, LANES)), 0.0)
            return jnp.sum(spread, axis=1, keepdims=True)

        upper = lax.broadcasted_iota(jnp.int32, (1, LANES), 1) < LANES // 2
        numerator = jnp.zeros((rows_each, HEAD_DIM), jnp.float32)
        denominator_row = jnp.zeros((1, LANES), jnp.float32)
        for piece, stat in zip(pieces, stats):
            factor = jnp.exp(jnp.where(upper, stat - top, LOW))
            numerator = numerator + piece * to_column(factor)
            sums = jnp.concatenate([stat[:, LANES // 2 :], stat[:, : LANES // 2]], axis=1)
            denominator_row = denominator_row + sums * factor
        top_column = to_column(top)
        denominator = to_column(denominator_row)
        group = line // GROUP
        start = (group * PER_KV + lax.rem(line, GROUP)) * 4 + b
        query = heads_all[step_index, pl.ds(start, rows_each, stride=4), :]
        new_at = (group * PER_KV + GROUP) * 4 + b
        new_scores = []
        new_values = []
        for past in range(step_index + 1):
            new_key = heads_all[past, pl.ds(new_at, 1), :]
            new_values.append(heads_all[past, pl.ds(new_at + 4, 1), :])
            new_scores.append(jnp.sum(query * new_key, axis=1, keepdims=True) * score_scale)
        peak = top_column
        for new_score in new_scores:
            peak = jnp.maximum(peak, new_score)
        factor = jnp.exp(top_column - peak)
        denominator = denominator * factor
        numerator = numerator * factor
        for new_score, new_value in zip(new_scores, new_values):
            weight = jnp.exp(new_score - peak)
            denominator = denominator + weight
            numerator = numerator + weight * new_value
        attended_own[step_index] = numerator / denominator
        for step in range(1, count):
            attended_copy(step_index, step).start()
        for place in range(rows_each):
            attended[step_index, line + place, pl.ds(b, 1), :] = attended_own[
                step_index, place : place + 1, :
            ]

    def share_copy(step_index, step):
        other = lax.rem(head + step, head_count)
        return pltpu.make_async_remote_copy(
            src_ref=share.at[step_index],
            dst_ref=share_arrived.at[step_index, head],
            send_sem=share_send_sem.at[step_index, step],
            recv_sem=share_sem.at[step_index, step],
            device_id=(me, other),
            device_id_type=MESH,
        )

    def project(step_index):
        others = arrived_attended(step_index)
        others.wait()
        lines = jnp.concatenate(
            [
                attended[step_index, pl.ds(place, out_chunks, stride=4), :, :].reshape(
                    out_chunks * 8, LANES
                )
                for place in range(4)
            ],
            axis=1,
        ).astype(jnp.bfloat16)
        moved = jnp.dot(lines, perm[...], preferred_element_type=jnp.float32)
        by_phase[...] = moved.reshape(out_chunks, 8, WIDE)

        def body(chunk, total):
            weights = jnp.concatenate([w_out[chunk, phase] for phase in range(4)], axis=1)
            return total + lax.dot_general(
                by_phase[chunk].astype(jnp.bfloat16),
                weights,
                NT,
                preferred_element_type=jnp.float32,
            )

        total = lax.fori_loop(0, out_chunks, body, jnp.zeros((8, depth), jnp.float32))
        scaled = total[0:batch, :] * (out_scale[...] / code_norm)
        share[step_index] = scaled
        share_arrived[step_index, head] = scaled
        for step in range(1, head_count):
            share_copy(step_index, step).start()
        for step in range(1, head_count):
            share_copy(step_index, step).wait_recv()
        update = share_arrived[step_index, 0]
        for other in range(1, head_count):
            update = update + share_arrived[step_index, other]
        fresh = (hidden[...] + update).astype(jnp.bfloat16)
        hidden[...] = fresh.astype(jnp.float32)

    def arrived_attended(step_index):
        class Waiter:
            def wait(self):
                spread = merge_arrived.at[step_index, pl.ds(1, count - 1), 0:rows_each, :]
                pltpu.make_async_copy(spread, spread, attended_sem.at[step_index]).wait()

        return Waiter()

    begin_step(0)
    qkv.first_windows()
    outs.begin()
    for b in range(batch):
        pltpu.make_async_copy(keys_hbm.at[b], keys.at[b], cache_sem.at[0, b]).start()
        pltpu.make_async_copy(values_hbm.at[b], values.at[b], cache_sem.at[1, b]).start()
    pl.semaphore_wait(barrier, count - 1 + head_count - 1)
    for step in range(1, count):
        square_copy(0, step).start()

    def beside(chunk, step, rows):
        before = jnp.maximum(chunk - 1, 0)
        weights = jnp.concatenate([w_qkv[before, phase, rows, :] for phase in range(4)], axis=1)
        product = jnp.dot(normed[:, rows], weights, preferred_element_type=jnp.float32)
        accum[...] += product

    def qkv_step(chunk, carry):
        accum[...] = jnp.zeros_like(accum)
        qkv.chunk(chunk, beside)
        part[0, chunk - 1] = accum[0:batch, :]
        send_part(0, chunk - 1)
        return carry

    qkv.chunk(0)
    lax.fori_loop(1, chunks, qkv_step, 0)
    part[0, chunks - 1] = qkv_product(chunks - 1)[0:batch, :]
    send_part(0, chunks - 1)
    marks = [0, out_chunks * 5 // 16, out_chunks * 10 // 16, out_chunks * 13 // 16, out_chunks]
    outs.first_windows()
    outs.run(marks[0], marks[1])
    finish_heads(0)
    outs.run(marks[1], marks[2])
    attend(0)
    outs.run(marks[2], marks[3])
    merge(0)
    outs.run(marks[3], marks[4])
    project(0)

    for step_index in range(1, DECODE_STEPS):
        begin_step(step_index)
        for step in range(1, count):
            square_copy(step_index, step).start()

        def again(chunk, carry):
            part[step_index, chunk] = qkv_product(chunk)[0:batch, :]
            send_part(step_index, chunk)
            return carry

        lax.fori_loop(0, chunks, again, 0)
        finish_heads(step_index)
        attend(step_index)
        merge(step_index)
        project(step_index)

    out_ref[...] = hidden[...].astype(jnp.bfloat16)

    for step_index in range(DECODE_STEPS):
        for step in range(1, count):
            square_copy(step_index, step).wait_send()
            merge_copy(step_index, step).wait_send()
            attended_copy(step_index, step).wait_send()
        for step in range(1, head_count):
            share_copy(step_index, step).wait_send()
        for chunk in range(chunks):

            @pl.when(me != chunk % count)
            def _(chunk=chunk):
                part_copy(step_index, chunk).wait_send()

            @pl.when(me == chunk % count)
            def _(chunk=chunk):
                for step in range(1, count):
                    heads_copy(step_index, chunk, step).wait_send()


def padded_codes(codes):
    extra = -codes.shape[1] % LANES
    return jnp.pad(codes, ((0, 0), (0, extra))) if extra else codes


def rope_tables(lengths):
    half = HEAD_DIM // 2
    lane = jnp.arange(LANES, dtype=jnp.int32) % TILE_BYTES
    phase = jnp.arange(4, dtype=jnp.int32)
    entry = 4 * lane[None, :] + phase[:, None]
    freqs = jnp.exp(
        -((entry % half).astype(jnp.float32) * (2.0 / HEAD_DIM)) * math.log(rope_base)
    )
    steps = jnp.arange(DECODE_STEPS, dtype=jnp.int32)
    positions = (lengths[None, :] + steps[:, None]).astype(jnp.float32)
    angles = positions[:, None, :, None] * freqs[None, :, None, :]
    sign = jnp.where(entry < half, -1.0, 1.0)[None, :, None, :]
    rows = ((0, 0), (0, 0), (0, 8 - lengths.shape[0]), (0, 0))
    return jnp.pad(jnp.cos(angles), rows), jnp.pad(jnp.sin(angles) * sign, rows)


def shards(
    hidden_in,
    norm_gain,
    qkv_codes,
    qkv_scale,
    out_codes,
    out_scale,
    cache_keys,
    cache_values,
    lengths,
):
    count = lax.axis_size("seq")
    head_count = lax.axis_size("head")
    batch, depth = hidden_in.shape
    qkv_codes = padded_codes(qkv_codes)
    out_codes = padded_codes(out_codes)
    chunks = qkv_codes.shape[1] // LANES
    out_chunks = out_codes.shape[1] // LANES
    extra = chunks * WIDE - qkv_scale.shape[0]
    if extra:
        qkv_scale = jnp.pad(qkv_scale, (0, extra))
    groups = cache_keys.shape[2]
    cached = cache_keys.shape[1] * groups
    head_rows = groups * GROUP
    rows_each = batch * head_rows // count
    owners = -(-chunks // count)
    cosine, sine = rope_tables(lengths)
    f32, bf16 = jnp.float32, jnp.bfloat16
    vmem = pl.BlockSpec(memory_space=pltpu.VMEM)
    hbm = pl.BlockSpec(memory_space=pl.ANY)
    steps = DECODE_STEPS
    dma = pltpu.SemaphoreType.DMA
    return pl.pallas_call(
        kernel,
        in_specs=[
            vmem, vmem, hbm, vmem, hbm, vmem, hbm, hbm,
            pl.BlockSpec(memory_space=pltpu.SMEM), vmem, vmem,
        ],
        out_specs=vmem,
        out_shape=jax.ShapeDtypeStruct((batch, depth), bf16),
        scratch_shapes=[
            pltpu.VMEM((chunks, 4, depth, LANES), bf16),
            pltpu.VMEM((out_chunks, 4, depth, LANES), bf16),
            pltpu.VMEM((DEPTH, depth, LANES), jnp.int32),
            pltpu.VMEM((2, depth, LANES), jnp.int32),
            pltpu.VMEM((DEPTH, depth, LANES), jnp.int32),
            pltpu.VMEM((2, depth, LANES), jnp.int32),
            pltpu.VMEM((batch, cached, HEAD_DIM), bf16),
            pltpu.VMEM((batch, cached, HEAD_DIM), bf16),
            pltpu.VMEM((WIDE, WIDE), bf16),
            pltpu.VMEM((16, depth), f32),
            pltpu.VMEM((16, depth), bf16),
            pltpu.VMEM((batch, depth), f32),
            pltpu.VMEM((16, WIDE), f32),
            pltpu.VMEM((steps, chunks, batch, WIDE), f32),
            pltpu.VMEM((16, WIDE), f32),
            pltpu.VMEM((owners, 8, WIDE), f32),
            pltpu.VMEM((steps, count, batch, LANES), f32),
            pltpu.VMEM((steps, owners, count - 1, batch, WIDE), f32),
            pltpu.VMEM((steps, chunks * 16, LANES), f32),
            pltpu.VMEM((2, head_rows, cached), f32),
            pltpu.VMEM((steps * count, rows_each + 1, LANES), f32),
            pltpu.VMEM((steps, count, rows_each + 1, LANES), f32),
            pltpu.VMEM((steps, head_rows, 8, LANES), f32),
            pltpu.VMEM((steps, rows_each, LANES), f32),
            pltpu.VMEM((out_chunks, 8, WIDE), f32),
            pltpu.VMEM((steps, batch, depth), f32),
            pltpu.VMEM((steps, head_count, batch, depth), f32),
            dma((DEPTH,)),
            dma((DEPTH,)),
            dma((2, batch)),
            dma((steps, count)),
            dma((steps, count)),
            dma((steps, chunks)),
            dma((steps, owners)),
            dma((steps, owners, count)),
            dma((steps, chunks)),
            dma((steps, count)),
            dma((steps, count)),
            dma((steps, count)),
            dma((steps,)),
            dma((steps, head_count)),
            dma((steps, head_count)),
        ],
        compiler_params=pltpu.CompilerParams(
            collective_id=0, has_side_effects=True, vmem_limit_bytes=66_000_000
        ),
    )(
        hidden_in,
        norm_gain[None, :],
        qkv_codes,
        qkv_scale[None, :],
        out_codes,
        out_scale[None, :],
        cache_keys.reshape(batch, cached, HEAD_DIM),
        cache_values.reshape(batch, cached, HEAD_DIM),
        lengths,
        cosine,
        sine,
    )


def solution(mesh):
    in_specs = (
        P(None, "seq"),
        P("seq"),
        P("seq", "head"),
        P("head"),
        P("seq", "head"),
        P("seq"),
        P(None, "seq", "head", None),
        P(None, "seq", "head", None),
        P(),
    )
    out_specs = P(None, "seq")
    return jax.shard_map(shards, mesh=mesh, in_specs=in_specs, out_specs=out_specs, check_vma=False)
```

time: 263 us -> 111 us (0.42)
  Pallas kernels: 161 us -> 107 us
  matrix products: 47.4 us -> 0 us
  local copies, waits for them, and re-layouts: 35.8 us -> 2.52 us
  other arithmetic: 10.7 us -> 0.88 us
  blocking collectives: 6.73 us -> 0 us
    pallas_call x6 -> x1, Pallas kernels: 161 us -> 107 us  [shards(): pl.pallas_call(kernel, in_specs=[vmem, vmem, hbm, vmem, hbm, vmem, hbm, h...]
    dot_general x8 -> x0, matrix products: 47.4 us -> none  [the longest x2 20.4 us: shards(): lax.dot_general(by_phase(attended, out_width), w_out, (((1,), (1,)), ((),...]
    reshape x6 -> x0, local copies, waits for them, and re-layouts: 16.4 us -> none  [the longest x2 10.2 us: from_phase(): return jnp.swapaxes(split, 1, 2).reshape(values.shape[0], 4 * count)]
    another operation x3 -> x0, local copies, waits for them, and re-layouts: 10.2 us -> none  [by_phase(): split = values.reshape(values.shape[:-1] + (values.shape[-1] // 4, 4))]
    psum x2 -> x0, blocking collectives: 6.73 us -> none  [shards(): update = lax.psum(update, 'head')]
    slice x6 -> x0, local copies, waits for them, and re-layouts: 4 us -> none  [the longest x2 2.14 us: merge_over_seq(): packed[..., HEAD_DIM]]
    concatenate x4 -> x0, other arithmetic: 3.03 us -> none  [the longest x2 1.64 us: merge_over_seq(): jnp.concatenate([local_acc, jnp.broadcast_to(local_max[..., None], half),...]
where the time goes in v1:
time: 111 us; the launch traced here: 110 us
  Pallas kernels  107 us (96%)
  local copies, waits for them, and re-layouts  2.52 us (2%)
    pallas_call x1, Pallas kernels, shards(): pl.pallas_call(kernel, in_specs=[vmem, vmem, hbm, vmem, hbm, vmem, hbm, h...  107 us

profile of v1, /device:TPU:0, one launch (start us, length us, event | category | flops | bytes accessed | tf_op | source)
XLA Modules:
  0.0 110.0 jit_solution(13980971896126797551)
XLA Ops:
  0.0 0.7 add_convert_fusion
  0.7 0.2 fusion
  0.9 0.6 pad.8.sine
  1.5 0.6 pad.7.cosine
  2.1 106.5 %shard_map.91 = bf16[4,1024]{1,0:T(4,128)(2,1)} custom-call(bf16[4,1024]{1,0:T(4,128)(2,1)} %hidden_ref.1, f32[1,1024]{1,0:T(1,128)} %bitcast.8, s32[1024,2304]{1,0:T(8,128)} %qkv_codes.1, f32[1,9216]{1,0:T(1,128)} %bitcast.7, s32[1024,2048]{1,0:T(8,128)} %out_codes.1, f32[1,1024]{1,0:T(1,128)} %bitcast.9, bf16[4,4096,128]{2,1,0:T(8,128)(2,1)} %bitcast.5, ...), custom_call_target="tpu_custom_call" | custom-call | tf_op jit(solution)/shard_map/pallas_call | solution.py:694
  108.7 1.3 %copy.11 = bf16[4,1024]{1,0:T(4,128)(2,1)} copy(bf16[4,1024]{1,0:T(4,128)(2,1)} %shard_map.91) | data formatting | bytes 16384
  (2 shorter events, 0.0 us)

commit v2 on v1

--- a/solution.py
+++ b/solution.py
@@ -23,22 +23,25 @@
 GROUP = HEADS // KV_HEADS
 PER_KV = GROUP + 2
 TILE_BYTES = TILE // 4
-ROWS = 128
-DEPTH = 3
+ROWS = 256
+SMALL = 128
+DEPTH = 4
 BYTES = 0x00FF00FF
 LOW = -1e30
 MESH = pl.DeviceIdType.MESH
 NT = (((1,), (1,)), ((), ()))
 
 
-def byte_windows(first):
-    lane = lax.broadcasted_iota(jnp.int32, first.shape, 1)
-    base = lane & ~(TILE_BYTES - 1)
-    one = base | ((lane + 1) & (TILE_BYTES - 1))
-    two = base | ((lane + 2) & (TILE_BYTES - 1))
-    second = jnp.take_along_axis(first, one, axis=1)
-    third = jnp.take_along_axis(first, two, axis=1)
-    return (((first << 8) | second) << 8) | third
+def window_matrix(turned):
+    row = lax.broadcasted_iota(jnp.int32, (LANES, LANES), 0)
+    lane = lax.broadcasted_iota(jnp.int32, (LANES, LANES), 1)
+    source, place = (lane, row) if turned else (row, lane)
+    base = place & ~(TILE_BYTES - 1)
+    one = base | ((place + 1) & (TILE_BYTES - 1))
+    two = base | ((place + 2) & (TILE_BYTES - 1))
+    matrix = jnp.where(source == place, 65536.0, 0.0)
+    matrix = matrix + jnp.where(source == one, 256.0, 0.0)
+    return (matrix + jnp.where(source == two, 1.0, 0.0)).astype(jnp.bfloat16)
 
 
 def hashed_weight(window, phase):
@@ -52,7 +55,8 @@
 
 
 class Stream:
-    def __init__(self, codes, buf, win, sem, weights):
+    def __init__(self, codes, buf, win, sem, weights, matrix):
+        self.matrix = matrix
         self.codes, self.buf, self.win, self.sem, self.weights = codes, buf, win, sem, weights
         self.count = codes.shape[1] // LANES
         self.rows = codes.shape[0]
@@ -77,11 +81,24 @@
         self.copy(0).wait()
 
         def body(step, carry):
-            rows = self.block_rows(step)
-            self.win[0, rows, :] = byte_windows(self.buf[0, rows, :])
+            self.form(0, 0, step)
             return carry
 
         lax.fori_loop(0, self.steps, body, 0)
+
+    def form(self, slot, place, step):
+        rows = self.block_rows(step)
+        codes = self.buf[slot, rows, :].astype(jnp.float32).astype(jnp.bfloat16)
+        window = jnp.dot(codes, self.matrix[...], preferred_element_type=jnp.float32)
+        self.win[place, rows, :] = window.astype(jnp.int32)
+
+    def hash(self, chunk, place, step):
+        small = math.gcd(self.block, SMALL)
+        for part in range(self.block // small):
+            rows = pl.ds(pl.multiple_of(step * self.block + part * small, small), small)
+            window = self.win[place, rows, :]
+            for phase in range(4):
+                self.weights[chunk, phase, rows, :] = hashed_weight(window, phase)
 
     def chunk(self, chunk, beside=None):
         now, later = lax.rem(chunk, 2), lax.rem(chunk + 1, 2)
@@ -96,13 +113,10 @@
             self.copy(chunk + DEPTH).start()
 
         def body(step, carry):
-            rows = self.block_rows(step)
             if beside is not None:
-                beside(chunk, step, rows)
-            window = self.win[now, rows, :]
-            for phase in range(4):
-                self.weights[chunk, phase, rows, :] = hashed_weight(window, phase)
-            self.win[later, rows, :] = byte_windows(self.buf[slot, rows, :])
+                beside(chunk, step, self.block_rows(step))
+            self.hash(chunk, now, step)
+            self.form(slot, later, step)
             return carry
 
         lax.fori_loop(0, self.steps, body, 0)
@@ -114,6 +128,30 @@
 
         if high > low:
             lax.fori_loop(low, high, body, 0)
+
+
+class TurnedStream(Stream):
+    def blocks(self, step):
+        for place in range(self.block // LANES):
+            yield step * (self.block // LANES) + place
+
+    def form(self, slot, place, step):
+        for block in self.blocks(step):
+            rows = pl.ds(pl.multiple_of(block * LANES, LANES), LANES)
+            codes = self.buf[slot, rows, :].astype(jnp.float32).astype(jnp.bfloat16)
+            window = lax.dot_general(
+                self.matrix[...], codes, NT, preferred_element_type=jnp.float32
+            )
+            self.win[place, rows, :] = window.astype(jnp.int32)
+
+    def hash(self, chunk, place, step):
+        for block in self.blocks(step):
+            for part in range(0, LANES, SMALL):
+                rows = pl.ds(pl.multiple_of(block * LANES + part, SMALL), SMALL)
+                window = self.win[place, rows, :]
+                for phase in range(4):
+                    lines = slice(phase * LANES + part, phase * LANES + part + SMALL)
+                    self.weights[chunk, block, lines, :] = hashed_weight(window, phase)
 
 
 def kernel(
@@ -126,8 +164,6 @@
     keys_hbm,
     values_hbm,
     lengths,
-    cosine,
-    sine,
     out_ref,
     w_qkv,
     w_out,
@@ -137,7 +173,10 @@
     out_win,
     keys,
     values,
+    cosine,
+    sine,
     perm,
+    windows,
     padded,
     normed,
     hidden,
@@ -191,9 +230,14 @@
     def peer(step):
         return lax.rem(me + step, count)
 
-    qkv = Stream(qkv_codes, qkv_buf, qkv_win, qkv_sem, w_qkv)
-    outs = Stream(out_codes, out_buf, out_win, out_sem, w_out)
+    def wait_bytes(ref, sem):
+        pltpu.make_async_copy(ref, ref, sem).wait()
+
+    qkv = Stream(qkv_codes, qkv_buf, qkv_win, qkv_sem, w_qkv, windows.at[0])
+    outs = TurnedStream(out_codes, out_buf, out_win, out_sem, w_out, windows.at[1])
     qkv.begin()
+    windows[0] = window_matrix(False)
+    windows[1] = window_matrix(True)
     barrier = pltpu.get_barrier_semaphore()
     for step in range(1, count):
         pl.semaphore_signal(barrier, inc=1, device_id=(peer(step), head), device_id_type=MESH)
@@ -214,6 +258,11 @@
     padded[...] = jnp.zeros_like(padded)
     attended[...] = jnp.zeros_like(attended)
     hidden[...] = hidden_ref[...].astype(jnp.float32)
+
+    for step in range(DECODE_STEPS):
+        for phase in range(4):
+            tables = rope_tables(lengths, batch, step, phase)
+            cosine[step, phase], sine[step, phase] = tables
 
     for index in range(owners):
         chunk = jnp.minimum(me + index * count, chunks - 1)
@@ -233,23 +282,12 @@
         )
     stage[...] = jnp.zeros_like(stage)
 
-    def start_square_copies(step_index):
-        for step in range(1, count):
-            pltpu.make_async_remote_copy(
-                src_ref=square_all.at[step_index, 0],
-                dst_ref=square_all.at[step_index, step],
-                send_sem=square_send_sem.at[step_index, step],
-                recv_sem=square_sem.at[step_index, step],
-                device_id=(peer(step), head),
-                device_id_type=MESH,
-            ).start()
-
     def square_copy(step_index, step):
         return pltpu.make_async_remote_copy(
             src_ref=square_all.at[step_index, 0],
             dst_ref=square_all.at[step_index, step],
-            send_sem=square_send_sem.at[step_index, step],
-            recv_sem=square_sem.at[step_index, step],
+            send_sem=square_send_sem.at[step_index],
+            recv_sem=square_sem.at[step_index],
             device_id=(peer(step), head),
             device_id_type=MESH,
         )
@@ -268,7 +306,7 @@
         return pltpu.make_async_remote_copy(
             src_ref=part.at[step_index, chunk],
             dst_ref=arrived.at[step_index, index, jnp.maximum(offset - 1, 0)],
-            send_sem=part_send_sem.at[step_index, chunk],
+            send_sem=part_send_sem.at[step_index],
             recv_sem=part_sem.at[step_index, index],
             device_id=(owner, head),
             device_id_type=MESH,
@@ -288,15 +326,14 @@
         return pltpu.make_async_remote_copy(
             src_ref=heads_all.at[step_index, rows, :],
             dst_ref=heads_all.at[step_index, rows, :],
-            send_sem=heads_send_sem.at[step_index, chunk // count, step],
-            recv_sem=heads_sem.at[step_index, chunk],
+            send_sem=heads_send_sem.at[step_index, chunk // count],
+            recv_sem=heads_sem.at[step_index],
             device_id=(peer(step), head),
             device_id_type=MESH,
         )
 
     def finish_heads(step_index):
-        for step in range(1, count):
-            square_copy(step_index, step).wait_recv()
+        wait_bytes(square_all.at[step_index, pl.ds(1, count - 1)], square_sem.at[step_index])
         squares = square_all[step_index, 0]
         for step in range(1, count):
             squares = squares + square_all[step_index, step]
@@ -307,8 +344,7 @@
             chunk = me + index * count
 
             def work(index=index, chunk=chunk):
-                pieces = arrived.at[step_index, index]
-                pltpu.make_async_copy(pieces, pieces, part_sem.at[step_index, index]).wait()
+                wait_bytes(arrived.at[step_index, index], part_sem.at[step_index, index])
                 total = part[step_index, chunk]
                 for step in range(count - 1):
                     total = total + arrived[step_index, index, step]
@@ -348,28 +384,51 @@
             else:
                 pl.when(chunk < chunks)(work)
 
+    def by_owned(action):
+        least = chunks // count
+        if chunks % count == 0:
+            action(least)
+        else:
+
+            @pl.when(me < chunks % count)
+            def _():
+                action(least + 1)
+
+            @pl.when(me >= chunks % count)
+            def _():
+                action(least)
+
     def wait_heads(step_index):
-        for chunk in range(chunks):
-
-            @pl.when(me != chunk % count)
-            def _(chunk=chunk):
-                heads_copy(step_index, chunk, 1).wait_recv()
+        def action(owned):
+            if chunks > owned:
+                rows = pl.ds(0, (chunks - owned) * 16)
+                wait_bytes(heads_all.at[step_index, rows, :], heads_sem.at[step_index])
+
+        by_owned(action)
+
+    def wait_part_sends(step_index):
+        def action(owned):
+            if chunks > owned:
+                sent = part.at[step_index, pl.ds(0, chunks - owned)]
+                wait_bytes(sent, part_send_sem.at[step_index])
+            for index in range(owned):
+                wait_bytes(arrived.at[step_index, index], heads_send_sem.at[step_index, index])
+
+        by_owned(action)
 
     def merge_copy(step_index, step):
         target = peer(step)
         return pltpu.make_async_remote_copy(
             src_ref=merge_send.at[step_index * count + target],
             dst_ref=merge_arrived.at[step_index, step],
-            send_sem=merge_send_sem.at[step_index, step],
-            recv_sem=merge_sem.at[step_index, step],
+            send_sem=merge_send_sem.at[step_index],
+            recv_sem=merge_sem.at[step_index],
             device_id=(target, head),
             device_id_type=MESH,
         )
 
     def attend(step_index):
         wait_heads(step_index)
-        column = lax.broadcasted_iota(jnp.int32, (head_rows, cached), 1)
-        row = lax.broadcasted_iota(jnp.int32, (head_rows, cached), 0)
         if step_index == 0:
             for b in range(batch):
                 pltpu.make_async_copy(keys_hbm.at[b], keys.at[b], cache_sem.at[0, b]).wait()
@@ -378,55 +437,93 @@
         tiles = cached // width
         lane = lax.broadcasted_iota(jnp.int32, (head_rows, LANES), 1)
         line = lax.broadcasted_iota(jnp.int32, (head_rows, LANES), 0)
-        for b in range(batch):
+        power = score_scale * math.log2(math.e)
+        blank = jnp.zeros((head_rows, HEAD_DIM), jnp.float32)
+
+        def over_lanes(block, combine):
+            result = block[:, :LANES]
+            for start in range(LANES, width, LANES):
+                result = combine(result, block[:, start : start + LANES])
+            return result
+
+        def mask(b, tile):
+            position = lax.broadcasted_iota(jnp.int32, (8, width), 1) + tile * width
+            live = position < (lengths[b] - me * block_len) * groups
+            for g in range(groups):
+                chosen = live & ((position & (groups - 1)) == g)
+                bias = jnp.where(chosen, 0.0, LOW)
+                yield jnp.concatenate([bias] * (GROUP // 8), axis=0)
+
+        for pair in range(batch // 2):
+            both = (2 * pair, 2 * pair + 1)
+            queries = [
+                jnp.concatenate(
+                    [
+                        heads_all[step_index, pl.ds(g * PER_KV * 4 + b, GROUP, stride=4), :]
+                        for g in range(groups)
+                    ],
+                    axis=0,
+                )
+                for b in both
+            ]
             query = jnp.concatenate(
                 [
-                    heads_all[step_index, pl.ds(g * PER_KV * 4 + b, GROUP, stride=4), :]
-                    for g in range(groups)
+                    jnp.concatenate([queries[0], blank], axis=1),
+                    jnp.concatenate([blank, queries[1]], axis=1),
                 ],
                 axis=0,
             ).astype(jnp.bfloat16)
-            live_length = lengths[b] - me * block_len
-            top = jnp.full((head_rows, 1), LOW, jnp.float32)
+            tops = [None] * (2 * groups)
             for tile in range(tiles):
                 columns = slice(tile * width, (tile + 1) * width)
-                score = (
-                    lax.dot_general(
-                        query, keys[b, columns, :], NT, preferred_element_type=jnp.float32
-                    )
-                    * score_scale
-                )
-                position = lax.broadcasted_iota(jnp.int32, (head_rows, width), 1) + tile * width
-                row_group = lax.broadcasted_iota(jnp.int32, (head_rows, width), 0) // GROUP
-                live = position < live_length * groups
-                if groups > 1:
-                    live = live & (lax.rem(position, groups) == row_group)
-                score = jnp.where(live, score, LOW)
-                scores[b % 2, :, columns] = score
-                top = jnp.maximum(top, jnp.max(score, axis=1, keepdims=True))
-            total = jnp.zeros((head_rows, 1), jnp.float32)
-            mixed = jnp.zeros((head_rows, HEAD_DIM), jnp.float32)
+                key = jnp.concatenate([keys[b, columns, :] for b in both], axis=1)
+                raw = lax.dot_general(query, key, NT, preferred_element_type=jnp.float32)
+                biases = [bias for b in both for bias in mask(b, tile)]
+                for place, bias in enumerate(biases):
+                    rows = slice(place * GROUP, (place + 1) * GROUP)
+                    masked = raw[rows, :] + bias
+                    scores[pair, rows, columns] = masked
+                    top = over_lanes(masked, jnp.maximum)
+                    tops[place] = top if tile == 0 else jnp.maximum(tops[place], top)
+            tops = [
+                jnp.maximum(jnp.max(top, axis=1, keepdims=True), 0.5 * LOW) for top in tops
+            ]
+            sums = [None] * (2 * groups)
+            mixed = jnp.zeros((2 * head_rows, 2 * HEAD_DIM), jnp.float32)
             for tile in range(tiles):
                 columns = slice(tile * width, (tile + 1) * width)
-                score = scores[b % 2, :, columns]
-                weight = jnp.where(score > 0.5 * LOW, jnp.exp(score - top), 0.0)
-                total = total + jnp.sum(weight, axis=1, keepdims=True)
+                weights = []
+                for place in range(2 * groups):
+                    rows = slice(place * GROUP, (place + 1) * GROUP)
+                    weight = jnp.exp2((scores[pair, rows, columns] - tops[place]) * power)
+                    part_sum = over_lanes(weight, jnp.add)
+                    sums[place] = part_sum if tile == 0 else sums[place] + part_sum
+                    weights.append(weight.astype(jnp.bfloat16))
+                value = jnp.concatenate([values[b, columns, :] for b in both], axis=1)
                 mixed = mixed + jnp.dot(
-                    weight.astype(jnp.bfloat16),
-                    values[b, columns, :],
-                    preferred_element_type=jnp.float32,
+                    jnp.concatenate(weights, axis=0), value, preferred_element_type=jnp.float32
                 )
-            spread = jnp.where(lane == line, top, 0.0) + jnp.where(
-                lane == line + LANES // 2, total, 0.0
-            )
-            spread = jnp.sum(spread, axis=0, keepdims=True)
-            each = head_rows // rows_each
-            for piece in range(each):
-                slot = step_index * count + b * each + piece
-                merge_send[slot, 0:rows_each, :] = mixed[
-                    piece * rows_each : (piece + 1) * rows_each, :
+            for side, b in enumerate(both):
+                mine = slice(side * groups, (side + 1) * groups)
+                top = jnp.concatenate(tops[mine], axis=0) * score_scale
+                total = jnp.concatenate(
+                    [jnp.sum(piece, axis=1, keepdims=True) for piece in sums[mine]], axis=0
+                )
+                spread = jnp.where(lane == line, top, 0.0) + jnp.where(
+                    lane == line + LANES // 2, total, 0.0
+                )
+                spread = jnp.sum(spread, axis=0, keepdims=True)
+                own = mixed[
+                    side * head_rows : (side + 1) * head_rows,
+                    side * HEAD_DIM : (side + 1) * HEAD_DIM,
                 ]
-                merge_send[slot, rows_each : rows_each + 1, :] = spread
+                each = head_rows // rows_each
+                for piece in range(each):
+                    slot = step_index * count + b * each + piece
+                    merge_send[slot, 0:rows_each, :] = own[
+                        piece * rows_each : (piece + 1) * rows_each, :
+                    ]
+                    merge_send[slot, rows_each : rows_each + 1, :] = spread
         for step in range(1, count):
             merge_copy(step_index, step).start()
 
@@ -441,15 +538,14 @@
         return pltpu.make_async_remote_copy(
             src_ref=attended_own.at[step_index],
             dst_ref=attended.at[step_index, pl.ds(line, rows_each), b, :],
-            send_sem=attended_send_sem.at[step_index, step],
+            send_sem=attended_send_sem.at[step_index],
             recv_sem=attended_sem.at[step_index],
             device_id=(peer(step), head),
             device_id_type=MESH,
         )
 
     def merge(step_index):
-        for step in range(1, count):
-            merge_copy(step_index, step).wait_recv()
+        wait_bytes(merge_arrived.at[step_index, pl.ds(1, count - 1)], merge_sem.at[step_index])
         b, line = attended_place()
         own = step_index * count + me
         pieces = [merge_send[own, 0:rows_each, :]]
@@ -511,15 +607,14 @@
         return pltpu.make_async_remote_copy(
             src_ref=share.at[step_index],
             dst_ref=share_arrived.at[step_index, head],
-            send_sem=share_send_sem.at[step_index, step],
-            recv_sem=share_sem.at[step_index, step],
+            send_sem=share_send_sem.at[step_index],
+            recv_sem=share_sem.at[step_index],
             device_id=(me, other),
             device_id_type=MESH,
         )
 
     def project(step_index):
-        others = arrived_attended(step_index)
-        others.wait()
+        wait_bytes(attended_bytes(step_index), attended_sem.at[step_index])
         lines = jnp.concatenate(
             [
                 attended[step_index, pl.ds(place, out_chunks, stride=4), :, :].reshape(
@@ -532,43 +627,41 @@
         moved = jnp.dot(lines, perm[...], preferred_element_type=jnp.float32)
         by_phase[...] = moved.reshape(out_chunks, 8, WIDE)
 
-        def body(chunk, total):
-            weights = jnp.concatenate([w_out[chunk, phase] for phase in range(4)], axis=1)
-            return total + lax.dot_general(
-                by_phase[chunk].astype(jnp.bfloat16),
-                weights,
-                NT,
-                preferred_element_type=jnp.float32,
-            )
-
-        total = lax.fori_loop(0, out_chunks, body, jnp.zeros((8, depth), jnp.float32))
+        together = max(size for size in (4, 2, 1) if out_chunks % size == 0)
+
+        def body(index, total):
+            for place in range(together):
+                chunk = index * together + place
+                weights = jnp.concatenate(
+                    [w_out[chunk, block] for block in range(depth // LANES)], axis=1
+                )
+                total = total + jnp.dot(
+                    by_phase[chunk].astype(jnp.bfloat16),
+                    weights,
+                    preferred_element_type=jnp.float32,
+                )
+            return total
+
+        blank = jnp.zeros((8, depth), jnp.float32)
+        total = lax.fori_loop(0, out_chunks // together, body, blank)
         scaled = total[0:batch, :] * (out_scale[...] / code_norm)
         share[step_index] = scaled
         share_arrived[step_index, head] = scaled
         for step in range(1, head_count):
             share_copy(step_index, step).start()
-        for step in range(1, head_count):
-            share_copy(step_index, step).wait_recv()
+        wait_bytes(share_arrived.at[step_index, pl.ds(0, head_count - 1)], share_sem.at[step_index])
         update = share_arrived[step_index, 0]
         for other in range(1, head_count):
             update = update + share_arrived[step_index, other]
         fresh = (hidden[...] + update).astype(jnp.bfloat16)
         hidden[...] = fresh.astype(jnp.float32)
 
-    def arrived_attended(step_index):
-        class Waiter:
-            def wait(self):
-                spread = merge_arrived.at[step_index, pl.ds(1, count - 1), 0:rows_each, :]
-                pltpu.make_async_copy(spread, spread, attended_sem.at[step_index]).wait()
-
-        return Waiter()
+    def attended_bytes(step_index):
+        return merge_arrived.at[step_index, pl.ds(1, count - 1), 0:rows_each, :]
 
     begin_step(0)
     qkv.first_windows()
     outs.begin()
-    for b in range(batch):
-        pltpu.make_async_copy(keys_hbm.at[b], keys.at[b], cache_sem.at[0, b]).start()
-        pltpu.make_async_copy(values_hbm.at[b], values.at[b], cache_sem.at[1, b]).start()
     pl.semaphore_wait(barrier, count - 1 + head_count - 1)
     for step in range(1, count):
         square_copy(0, step).start()
@@ -590,7 +683,10 @@
     lax.fori_loop(1, chunks, qkv_step, 0)
     part[0, chunks - 1] = qkv_product(chunks - 1)[0:batch, :]
     send_part(0, chunks - 1)
-    marks = [0, out_chunks * 5 // 16, out_chunks * 10 // 16, out_chunks * 13 // 16, out_chunks]
+    for b in range(batch):
+        pltpu.make_async_copy(keys_hbm.at[b], keys.at[b], cache_sem.at[0, b]).start()
+        pltpu.make_async_copy(values_hbm.at[b], values.at[b], cache_sem.at[1, b]).start()
+    marks = [0, out_chunks * 3 // 16, out_chunks * 7 // 16, out_chunks * 12 // 16, out_chunks]
     outs.first_windows()
     outs.run(marks[0], marks[1])
     finish_heads(0)
@@ -606,12 +702,17 @@
         for step in range(1, count):
             square_copy(step_index, step).start()
 
-        def again(chunk, carry):
-            part[step_index, chunk] = qkv_product(chunk)[0:batch, :]
-            send_part(step_index, chunk)
+        together = max(size for size in (3, 2, 1) if chunks % size == 0)
+
+        def again(index, carry):
+            several = [index * together + place for place in range(together)]
+            for chunk, product in zip(several, [qkv_product(chunk) for chunk in several]):
+                part[step_index, chunk] = product[0:batch, :]
+            for chunk in several:
+                send_part(step_index, chunk)
             return carry
 
-        lax.fori_loop(0, chunks, again, 0)
+        lax.fori_loop(0, chunks // together, again, 0)
         finish_heads(step_index)
         attend(step_index)
         merge(step_index)
@@ -620,43 +721,33 @@
     out_ref[...] = hidden[...].astype(jnp.bfloat16)
 
     for step_index in range(DECODE_STEPS):
-        for step in range(1, count):
-            square_copy(step_index, step).wait_send()
-            merge_copy(step_index, step).wait_send()
-            attended_copy(step_index, step).wait_send()
-        for step in range(1, head_count):
-            share_copy(step_index, step).wait_send()
-        for chunk in range(chunks):
-
-            @pl.when(me != chunk % count)
-            def _(chunk=chunk):
-                part_copy(step_index, chunk).wait_send()
-
-            @pl.when(me == chunk % count)
-            def _(chunk=chunk):
-                for step in range(1, count):
-                    heads_copy(step_index, chunk, step).wait_send()
+        others = pl.ds(1, count - 1)
+        wait_bytes(square_all.at[step_index, others], square_send_sem.at[step_index])
+        wait_bytes(merge_arrived.at[step_index, others], merge_send_sem.at[step_index])
+        wait_bytes(attended_bytes(step_index), attended_send_sem.at[step_index])
+        heads_away = share_arrived.at[step_index, pl.ds(0, head_count - 1)]
+        wait_bytes(heads_away, share_send_sem.at[step_index])
+        wait_part_sends(step_index)
+
+
+def rope_tables(lengths, batch, step, phase):
+    half = HEAD_DIM // 2
+    row = lax.broadcasted_iota(jnp.int32, (8, LANES), 0)
+    lane = lax.broadcasted_iota(jnp.int32, (8, LANES), 1)
+    entry = 4 * (lane & (TILE_BYTES - 1)) + phase
+    place = (entry & (half - 1)).astype(jnp.float32)
+    freqs = jnp.exp(-(place * (2.0 / HEAD_DIM)) * math.log(rope_base))
+    position = jnp.zeros((8, LANES), jnp.int32)
+    for b in range(batch):
+        position = jnp.where(row == b, lengths[b] + step, position)
+    angle = position.astype(jnp.float32) * freqs
+    sine = jnp.sin(angle)
+    return jnp.cos(angle), jnp.where(entry < half, -sine, sine)
 
 
 def padded_codes(codes):
     extra = -codes.shape[1] % LANES
     return jnp.pad(codes, ((0, 0), (0, extra))) if extra else codes
-
-
-def rope_tables(lengths):
-    half = HEAD_DIM // 2
-    lane = jnp.arange(LANES, dtype=jnp.int32) % TILE_BYTES
-    phase = jnp.arange(4, dtype=jnp.int32)
-    entry = 4 * lane[None, :] + phase[:, None]
-    freqs = jnp.exp(
-        -((entry % half).astype(jnp.float32) * (2.0 / HEAD_DIM)) * math.log(rope_base)
-    )
-    steps = jnp.arange(DECODE_STEPS, dtype=jnp.int32)
-    positions = (lengths[None, :] + steps[:, None]).astype(jnp.float32)
-    angles = positions[:, None, :, None] * freqs[None, :, None, :]
-    sign = jnp.where(entry < half, -1.0, 1.0)[None, :, None, :]
-    rows = ((0, 0), (0, 0), (0, 8 - lengths.shape[0]), (0, 0))
-    return jnp.pad(jnp.cos(angles), rows), jnp.pad(jnp.sin(angles) * sign, rows)
 
 
 def shards(
@@ -685,7 +776,6 @@
     head_rows = groups * GROUP
     rows_each = batch * head_rows // count
     owners = -(-chunks // count)
-    cosine, sine = rope_tables(lengths)
     f32, bf16 = jnp.float32, jnp.bfloat16
     vmem = pl.BlockSpec(memory_space=pltpu.VMEM)
     hbm = pl.BlockSpec(memory_space=pl.ANY)
@@ -695,20 +785,23 @@
         kernel,
         in_specs=[
             vmem, vmem, hbm, vmem, hbm, vmem, hbm, hbm,
-            pl.BlockSpec(memory_space=pltpu.SMEM), vmem, vmem,
+            pl.BlockSpec(memory_space=pltpu.SMEM),
         ],
         out_specs=vmem,
         out_shape=jax.ShapeDtypeStruct((batch, depth), bf16),
         scratch_shapes=[
             pltpu.VMEM((chunks, 4, depth, LANES), bf16),
-            pltpu.VMEM((out_chunks, 4, depth, LANES), bf16),
+            pltpu.VMEM((out_chunks, depth // LANES, WIDE, LANES), bf16),
             pltpu.VMEM((DEPTH, depth, LANES), jnp.int32),
             pltpu.VMEM((2, depth, LANES), jnp.int32),
             pltpu.VMEM((DEPTH, depth, LANES), jnp.int32),
             pltpu.VMEM((2, depth, LANES), jnp.int32),
             pltpu.VMEM((batch, cached, HEAD_DIM), bf16),
             pltpu.VMEM((batch, cached, HEAD_DIM), bf16),
+            pltpu.VMEM((steps, 4, 8, LANES), f32),
+            pltpu.VMEM((steps, 4, 8, LANES), f32),
             pltpu.VMEM((WIDE, WIDE), bf16),
+            pltpu.VMEM((2, LANES, LANES), bf16),
             pltpu.VMEM((16, depth), f32),
             pltpu.VMEM((16, depth), bf16),
             pltpu.VMEM((batch, depth), f32),
@@ -719,7 +812,7 @@
             pltpu.VMEM((steps, count, batch, LANES), f32),
             pltpu.VMEM((steps, owners, count - 1, batch, WIDE), f32),
             pltpu.VMEM((steps, chunks * 16, LANES), f32),
-            pltpu.VMEM((2, head_rows, cached), f32),
+            pltpu.VMEM((batch // 2, 2 * head_rows, cached), f32),
             pltpu.VMEM((steps * count, rows_each + 1, LANES), f32),
             pltpu.VMEM((steps, count, rows_each + 1, LANES), f32),
             pltpu.VMEM((steps, head_rows, 8, LANES), f32),
@@ -730,18 +823,18 @@
             dma((DEPTH,)),
             dma((DEPTH,)),
             dma((2, batch)),
-            dma((steps, count)),
-            dma((steps, count)),
-            dma((steps, chunks)),
+            dma((steps,)),
+            dma((steps,)),
+            dma((steps,)),
             dma((steps, owners)),
-            dma((steps, owners, count)),
-            dma((steps, chunks)),
-            dma((steps, count)),
-            dma((steps, count)),
-            dma((steps, count)),
-            dma((steps,)),
-            dma((steps, head_count)),
-            dma((steps, head_count)),
+            dma((steps, owners)),
+            dma((steps,)),
+            dma((steps,)),
+            dma((steps,)),
+            dma((steps,)),
+            dma((steps,)),
+            dma((steps,)),
+            dma((steps,)),
         ],
         compiler_params=pltpu.CompilerParams(
             collective_id=0, has_side_effects=True, vmem_limit_bytes=66_000_000
@@ -756,8 +849,6 @@
         cache_keys.reshape(batch, cached, HEAD_DIM),
         cache_values.reshape(batch, cached, HEAD_DIM),
         lengths,
-        cosine,
-        sine,
     )
 
 

time: 111 us -> 87.5 us (0.79)
  Pallas kernels: 107 us -> 85.9 us
  local copies, waits for them, and re-layouts: 2.52 us -> 1.3 us
    pallas_call x1, Pallas kernels: 107 us -> 85.9 us  [shards(): pl.pallas_call(kernel, in_specs=[vmem, vmem, hbm, vmem, hbm, vmem, hbm, h...]
    pad x2 -> x0, local copies, waits for them, and re-layouts: 1.22 us -> none  [the longest x1 0.61 us: rope_tables(): jnp.pad(jnp.sin(angles) * sign, rows)]
where the time goes in v2:
time: 87.5 us; the launch traced here: 87.2 us
  Pallas kernels  85.9 us (98%)
  local copies, waits for them, and re-layouts  1.3 us (1%)
    pallas_call x1, Pallas kernels, shards(): pl.pallas_call(kernel, in_specs=[vmem, vmem, hbm, vmem, hbm, vmem, hbm, h...  85.9 us

profile of v2, /device:TPU:0, one launch (start us, length us, event | category | flops | bytes accessed | tf_op | source)
XLA Modules:
  0.0 87.2 jit_solution(9718883375984027676)
XLA Ops:
  0.0 85.9 %shard_map.91 = bf16[4,1024]{1,0:T(4,128)(2,1)} custom-call(bf16[4,1024]{1,0:T(4,128)(2,1)} %hidden_ref.1, f32[1,1024]{1,0:T(1,128)} %bitcast.8, s32[1024,2304]{1,0:T(8,128)} %qkv_codes.1, f32[1,9216]{1,0:T(1,128)} %bitcast.7, s32[1024,2048]{1,0:T(8,128)} %out_codes.1, f32[1,1024]{1,0:T(1,128)} %bitcast.9, bf16[4,4096,128]{2,1,0:T(8,128)(2,1)} %bitcast.5, ...), custom_call_target="tpu_custom_call" | custom-call | tf_op jit(solution)/shard_map/pallas_call | solution.py:784
  85.9 1.3 %copy.11 = bf16[4,1024]{1,0:T(4,128)(2,1)} copy(bf16[4,1024]{1,0:T(4,128)(2,1)} %shard_map.91) | data formatting | bytes 16384
